TPU v7x, 32 devices: a whole 2x2x4 slice. The times are simulated.
32 devices in a mesh: cp: 8 (over y, x, core), tp: 4 (over z).
Axes of the slice: x: 2, y: 2, z: 4, core: 2. Of those that a mesh axis runs over, the one named last changes fastest.
Arguments:
- queries: bfloat16 [6144, 5120], P('cp', 'tp'), may hold values from -36 to 36
- keys: bfloat16 [6144, 1024], P('cp', 'tp'), may hold values from -5 to 5
- values: bfloat16 [6144, 1024], P('cp', 'tp'), may hold values from -6 to 6
- doc_lengths: int32 [8], replicated, may hold values from 1 to 1536, 6144 in all
Outputs:
- attended: bfloat16 [6144, 5120], P(('cp', 'tp'))
Inputs may be any that keep to these rules, and one draw needn't show every extreme that they name: `doc_lengths`: they sum to 6144, and one of them is exactly 1536.
All inputs are finite; a program needn't handle non-finite values.
Results may differ from a plain program's by a relative error of at most 0.0038.
Values may be sent and summed in bfloat16 or wider, within the bound.
A program may use at most 256 MiB of HBM per device.

v0:
```python
import jax
import jax.numpy as jnp
from jax import lax
from jax.sharding import PartitionSpec as P

HEAD = 128
DOC_DEVS = 2
negative = -1e30


def doc_index(positions, doc_ends):
    return jnp.sum((positions[..., None] >= doc_ends).astype(jnp.int32), axis=-1)


def on_device(queries, keys, values, doc_lengths):
    tok_rows, q_cols = queries.shape
    kv_cols = keys.shape[1]
    kv_local = kv_cols // HEAD
    group_size = q_cols // kv_cols
    half_rows = tok_rows // 2
    cp_size = lax.axis_size("cp")
    my_index = lax.axis_index("cp")
    stretch_span = 2 * min(DOC_DEVS, cp_size // 2)
    doc_ends = jnp.cumsum(doc_lengths)
    paired = jnp.stack([keys, values])
    kv_bank = lax.all_gather(paired[None], "cp", axis=0, tiled=True)
    bank_slots = kv_bank.shape[0]
    kv_bank = kv_bank.reshape(bank_slots, 2, 2, half_rows, kv_local, HEAD)
    stretch_ids = jnp.stack([my_index, 2 * cp_size - 1 - my_index])
    offsets = jnp.arange(half_rows, dtype=jnp.int32)
    q_pos = stretch_ids[:, None] * half_rows + offsets[None, :]
    q_doc = doc_index(q_pos, doc_ends)
    q_blocks = queries.reshape(2, half_rows, kv_local, group_size, HEAD)
    scale = float(HEAD) ** (-0.5)

    def fetch_block(kv_slot, kv_part):
        kv_piece = lax.dynamic_index_in_dim(kv_bank, kv_slot, 0, keepdims=False)
        return lax.dynamic_index_in_dim(kv_piece, kv_part, 1, keepdims=False)

    def one_tile(tile_step, state_now):
        needed = stretch_ids - tile_step
        present = needed >= 0
        clamped = jnp.maximum(needed, 0)
        device_ids = jnp.where(clamped < cp_size, clamped, 2 * cp_size - 1 - clamped)
        kv_part = (clamped >= cp_size).astype(jnp.int32)
        kv_slot = jnp.clip(device_ids, 0, bank_slots - 1)
        k_pos = clamped[:, None] * half_rows + offsets[None, :]
        k_doc = doc_index(k_pos, doc_ends)
        allowed = (
            present[:, None, None]
            & (k_doc[:, None, :] == q_doc[:, :, None])
            & (k_pos[:, None, :] <= q_pos[:, :, None])
        )
        running_max, running_sum, running_out = state_now
        pieces = jnp.stack([fetch_block(kv_slot[which], kv_part[which]) for which in range(2)])
        scores = (
            jnp.einsum(
                "cqhjd,ckhd->cqhjk", q_blocks, pieces[:, 0], preferred_element_type=jnp.float32
            )
            * scale
        )
        allowed_wide = allowed[:, :, None, None, :]
        scores = jnp.where(allowed_wide, scores, negative)
        new_max = jnp.maximum(running_max, jnp.max(scores, axis=-1))
        weights = jnp.where(allowed_wide, jnp.exp(scores - new_max[..., None]), 0.0)
        rescale = jnp.exp(running_max - new_max)
        new_sum = rescale * running_sum + jnp.sum(weights, axis=-1)
        product = jnp.einsum(
            "cqhjk,ckhd->cqhjd",
            weights.astype(jnp.bfloat16),
            pieces[:, 1],
            preferred_element_type=jnp.float32,
        )
        new_out = rescale[..., None] * running_out + product
        return (new_max, new_sum, new_out)

    start_state = (
        jnp.full((2, half_rows, kv_local, group_size), negative, jnp.float32),
        jnp.zeros((2, half_rows, kv_local, group_size), jnp.float32),
        jnp.zeros((2, half_rows, kv_local, group_size, HEAD), jnp.float32),
    )
    final_max, final_sum, final_out = lax.fori_loop(0, stretch_span + 1, one_tile, start_state)
    attended = (final_out / final_sum[..., None]).reshape(tok_rows, q_cols).astype(jnp.bfloat16)
    return lax.all_to_all(attended, "tp", split_axis=0, concat_axis=1, tiled=True)


def solution(mesh):
    in_specs = (P("cp", "tp"), P("cp", "tp"), P("cp", "tp"), P())
    out_specs = P(("cp", "tp"), None)
    return jax.shard_map(
        on_device, mesh=mesh, in_specs=in_specs, out_specs=out_specs, check_vma=False
    )
```

profile of v0, /device:TPU:0, one launch (start us, length us, event | category | flops | bytes accessed | tf_op | source)
XLA Modules:
  0.0 252.6 jit_solution(6885560735671889990)
XLA Ops:
  6.5 0.0 all-gather.3.cloned.1.call-start
  6.5 2.1 pad_maximum_fusion.1
  8.6 0.0 all-gather.3.cloned.1.call-update
  8.7 0.8 reduce-window.8
  9.5 5.7 %reshape.167 = bf16[2,384,2,5,128]{4,3,2,1,0:T(8,128)(2,1)} reshape(bf16[768,1280]{1,0:T(8,128)(2,1)} %param.6) | data formatting | bytes 3932160 | tf_op jit(solution)/shard_map/reshape | solution.py:33
  15.2 2.4 copy.32
  17.6 0.1 broadcast_multiply_fusion.1
  17.7 0.1 iota_add_fusion.2
  17.8 0.1 convert_reduce_fusion.1
  17.9 39.5 %all-gather.3.cloned.1.call-done = bf16[16,768,256]{2,1,0:T(8,128)(2,1)} async-done(((bf16[2,768,256]{2,1,0:T(8,128)(2,1)}), bf16[16,768,256]{2,1,0:T(8,128)(2,1)}) %all-gather.3.cloned.1.call-update) | async-done | bytes 6291472 | tf_op jit(solution)/shard_map/all_gather | solution.py:26
  57.4 9.8 %reshape.161 = bf16[8,2,2,384,2,128]{5,4,3,2,1,0:T(2,128)(2,1)} reshape(bf16[16,768,256]{2,1,0:T(8,128)(2,1)} %all-gather.3.cloned.1.call-done) | data formatting | bytes 12582912 | tf_op jit(solution)/shard_map/reshape | solution.py:28
  67.1 7.1 %copy.31 = bf16[8,2,2,384,2,128]{5,3,4,1,2,0:T(8,128)(2,1)} copy(bf16[8,2,2,384,2,128]{5,4,3,2,1,0:T(2,128)(2,1)} %reshape.161) | data formatting | bytes 12582912
  74.2 108.8 %while.21 = (s32[]{:T(128)}, f32[2,384,2,5]{1,3,2,0:T(8,128)S(1)}, f32[2,384,2,5]{1,3,2,0:T(8,128)S(1)}, f32[2,384,2,5,128]{1,4,3,2,0:T(8,128)}, s32[2]{0:T(128)...) while((s32[]{:T(128)}, f32[2,384,2,5]{1,3,2,0:T(8,128)S(1)}, ...), condition=%wide.region_6.7_spmd.clone, body=%wide.region_2.6_spmd.clone.sunk | while | flops 1554047232 | bytes 50061820 | solution.py:82
  74.2 0.6 fusion.41
  78.5 0.6 fusion.40
  82.7 0.1 iota_add_fusion.4
  82.8 0.1 convert_reduce_fusion.3
  82.9 0.4 compare_and_fusion.2
  83.3 1.2 dynamic-slice_bitcast_fusion.3
  84.5 2.0 fusion.42
  86.5 2.9 %fusion.43 = f32[2,384,2,5]{1,3,2,0:T(8,128)S(1)} fusion(f32[2,2,384,384,5]{3,2,4,1,0:T(8,128)S(1)} %get-tuple-element.508, f32[2,384,2,5]{1,3,2,0:T(8,128)S(1)} %select_maximum_fusion.2, pred[2,384,384]{1,2,0:T(8,128)(4,1)S(1)} %compare_and_fusion.2), kind=kLoop, calls=%fused_computation.6.clone.1 | loop fusion | flops 14737920 | bytes 12152832 | tf_op jit(solution)/shard_map/while/body/eval_jaxpr/reduce_sum | solution.py:67
  89.4 5.3 %bitcast_add_fusion.2 = f32[2,384,2,5,128]{1,4,3,2,0:T(8,128)} fusion(f32[2,384,2,5,128]{1,4,3,2,0:T(8,128)} %get-tuple-element.529, f32[2,2,384,384,5]{3,2,4,1,0:T(8,128)S(1)} %get-tuple-element.508, f32[2,384,2,5]{1,3,2,0:T(8,128)S(1)} %select_maximum_fusion.2, pred[2,384,384]{1,2,0:T(8,128)(4,1)S(1)} %compare_and_fusion.2, ...), kind=kOutput, calls=%fused_computation.9.clone.1 | convolution fusion | flops 773455872 | bytes 20803584 | tf_op jit(solution)/shard_map/while/body/eval_jaxpr/cqhjk,ckhd->cqhjd/dot_general | solution.py:68
  94.8 0.6 fusion.41
  99.0 0.6 fusion.40
  103.3 0.1 iota_add_fusion.4
  103.4 0.1 convert_reduce_fusion.3
  103.4 0.4 compare_and_fusion.2
  103.8 1.2 dynamic-slice_bitcast_fusion.3
  105.0 2.0 fusion.42
  107.1 2.9 %fusion.43 = f32[2,384,2,5]{1,3,2,0:T(8,128)S(1)} fusion(f32[2,2,384,384,5]{3,2,4,1,0:T(8,128)S(1)} %get-tuple-element.508, f32[2,384,2,5]{1,3,2,0:T(8,128)S(1)} %select_maximum_fusion.2, pred[2,384,384]{1,2,0:T(8,128)(4,1)S(1)} %compare_and_fusion.2), kind=kLoop, calls=%fused_computation.6.clone.1 | loop fusion | flops 14737920 | bytes 12152832 | tf_op jit(solution)/shard_map/while/body/eval_jaxpr/reduce_sum | solution.py:67
  110.0 6.8 %bitcast_add_fusion.2 = f32[2,384,2,5,128]{1,4,3,2,0:T(8,128)} fusion(f32[2,384,2,5,128]{1,4,3,2,0:T(8,128)} %get-tuple-element.529, f32[2,2,384,384,5]{3,2,4,1,0:T(8,128)S(1)} %get-tuple-element.508, f32[2,384,2,5]{1,3,2,0:T(8,128)S(1)} %select_maximum_fusion.2, pred[2,384,384]{1,2,0:T(8,128)(4,1)S(1)} %compare_and_fusion.2, ...), kind=kOutput, calls=%fused_computation.9.clone.1 | convolution fusion | flops 773455872 | bytes 20803584 | tf_op jit(solution)/shard_map/while/body/eval_jaxpr/cqhjk,ckhd->cqhjd/dot_general | solution.py:68
  116.8 0.6 fusion.41
  121.1 0.6 fusion.40
  125.3 0.1 iota_add_fusion.4
  125.4 0.1 convert_reduce_fusion.3
  125.5 0.4 compare_and_fusion.2
  125.9 1.2 dynamic-slice_bitcast_fusion.3
  127.1 2.0 fusion.42
  129.1 2.9 %fusion.43 = f32[2,384,2,5]{1,3,2,0:T(8,128)S(1)} fusion(f32[2,2,384,384,5]{3,2,4,1,0:T(8,128)S(1)} %get-tuple-element.508, f32[2,384,2,5]{1,3,2,0:T(8,128)S(1)} %select_maximum_fusion.2, pred[2,384,384]{1,2,0:T(8,128)(4,1)S(1)} %compare_and_fusion.2), kind=kLoop, calls=%fused_computation.6.clone.1 | loop fusion | flops 14737920 | bytes 12152832 | tf_op jit(solution)/shard_map/while/body/eval_jaxpr/reduce_sum | solution.py:67
  132.1 6.8 %bitcast_add_fusion.2 = f32[2,384,2,5,128]{1,4,3,2,0:T(8,128)} fusion(f32[2,384,2,5,128]{1,4,3,2,0:T(8,128)} %get-tuple-element.529, f32[2,2,384,384,5]{3,2,4,1,0:T(8,128)S(1)} %get-tuple-element.508, f32[2,384,2,5]{1,3,2,0:T(8,128)S(1)} %select_maximum_fusion.2, pred[2,384,384]{1,2,0:T(8,128)(4,1)S(1)} %compare_and_fusion.2, ...), kind=kOutput, calls=%fused_computation.9.clone.1 | convolution fusion | flops 773455872 | bytes 20803584 | tf_op jit(solution)/shard_map/while/body/eval_jaxpr/cqhjk,ckhd->cqhjd/dot_general | solution.py:68
  138.9 0.6 fusion.41
  143.2 0.6 fusion.40
  147.4 0.1 iota_add_fusion.4
  147.5 0.1 convert_reduce_fusion.3
  147.6 0.4 compare_and_fusion.2
  148.0 1.2 dynamic-slice_bitcast_fusion.3
  149.1 2.0 fusion.42
  151.2 2.9 %fusion.43 = f32[2,384,2,5]{1,3,2,0:T(8,128)S(1)} fusion(f32[2,2,384,384,5]{3,2,4,1,0:T(8,128)S(1)} %get-tuple-element.508, f32[2,384,2,5]{1,3,2,0:T(8,128)S(1)} %select_maximum_fusion.2, pred[2,384,384]{1,2,0:T(8,128)(4,1)S(1)} %compare_and_fusion.2), kind=kLoop, calls=%fused_computation.6.clone.1 | loop fusion | flops 14737920 | bytes 12152832 | tf_op jit(solution)/shard_map/while/body/eval_jaxpr/reduce_sum | solution.py:67
  154.1 6.8 %bitcast_add_fusion.2 = f32[2,384,2,5,128]{1,4,3,2,0:T(8,128)} fusion(f32[2,384,2,5,128]{1,4,3,2,0:T(8,128)} %get-tuple-element.529, f32[2,2,384,384,5]{3,2,4,1,0:T(8,128)S(1)} %get-tuple-element.508, f32[2,384,2,5]{1,3,2,0:T(8,128)S(1)} %select_maximum_fusion.2, pred[2,384,384]{1,2,0:T(8,128)(4,1)S(1)} %compare_and_fusion.2, ...), kind=kOutput, calls=%fused_computation.9.clone.1 | convolution fusion | flops 773455872 | bytes 20803584 | tf_op jit(solution)/shard_map/while/body/eval_jaxpr/cqhjk,ckhd->cqhjd/dot_general | solution.py:68
  161.0 0.6 fusion.41
  165.2 0.6 fusion.40
  169.5 0.1 iota_add_fusion.4
  169.5 0.1 convert_reduce_fusion.3
  169.6 0.4 compare_and_fusion.2
  170.0 1.2 dynamic-slice_bitcast_fusion.3
  171.2 2.0 fusion.42
  173.3 2.9 %fusion.43 = f32[2,384,2,5]{1,3,2,0:T(8,128)S(1)} fusion(f32[2,2,384,384,5]{3,2,4,1,0:T(8,128)S(1)} %get-tuple-element.508, f32[2,384,2,5]{1,3,2,0:T(8,128)S(1)} %select_maximum_fusion.2, pred[2,384,384]{1,2,0:T(8,128)(4,1)S(1)} %compare_and_fusion.2), kind=kLoop, calls=%fused_computation.6.clone.1 | loop fusion | flops 14737920 | bytes 12152832 | tf_op jit(solution)/shard_map/while/body/eval_jaxpr/reduce_sum | solution.py:67
  176.2 6.8 %bitcast_add_fusion.2 = f32[2,384,2,5,128]{1,4,3,2,0:T(8,128)} fusion(f32[2,384,2,5,128]{1,4,3,2,0:T(8,128)} %get-tuple-element.529, f32[2,2,384,384,5]{3,2,4,1,0:T(8,128)S(1)} %get-tuple-element.508, f32[2,384,2,5]{1,3,2,0:T(8,128)S(1)} %select_maximum_fusion.2, pred[2,384,384]{1,2,0:T(8,128)(4,1)S(1)} %compare_and_fusion.2, ...), kind=kOutput, calls=%fused_computation.9.clone.1 | convolution fusion | flops 773455872 | bytes 20803584 | tf_op jit(solution)/shard_map/while/body/eval_jaxpr/cqhjk,ckhd->cqhjd/dot_general | solution.py:68
  183.0 3.8 %divide_convert_fusion = bf16[2,384,2,5,128]{1,4,3,2,0:T(8,128)(2,1)} fusion(f32[2,384,2,5,128]{1,4,3,2,0:T(8,128)} %get-tuple-element.300, f32[2,384,2,5]{1,3,2,0:T(8,128)S(1)} %get-tuple-element.301), kind=kLoop, calls=%fused_computation.40 | loop fusion | flops 1966080 | bytes 5928960 | tf_op jit(solution)/shard_map/convert_element_type | solution.py:83
  186.8 3.8 %copy.41 = bf16[2,384,2,5,128]{4,3,2,1,0:T(8,128)(2,1)S(1)} copy(bf16[2,384,2,5,128]{1,4,3,2,0:T(8,128)(2,1)} %divide_convert_fusion) | data formatting | bytes 3932160 | tf_op jit(solution)/shard_map/convert_element_type | solution.py:83
  190.7 3.2 %reshape.168 = bf16[4,192,1280]{2,1,0:T(8,128)(2,1)} reshape(bf16[2,384,2,5,128]{4,3,2,1,0:T(8,128)(2,1)S(1)} %copy.41) | data formatting | bytes 3932160 | tf_op jit(solution)/shard_map/convert_element_type | solution.py:83
  193.9 50.4 %all_to_all.16 = bf16[4,192,1280]{2,1,0:T(8,128)(2,1)S(1)} all-to-all(bf16[4,192,1280]{2,1,0:T(8,128)(2,1)} %reshape.168), channel_id=1, replica_groups=mesh['cp'=8,'tp'=4] {'tp'}, dimensions={0} | all-to-all | bytes 3932160 | tf_op jit(solution)/shard_map/all_to_all | solution.py:84
  244.3 1.5 copy.45
  (28 shorter events, 0.4 us)
Async XLA Ops:
  6.5 50.8 %all-gather.3.cloned.1.call-start = ((), (), s32[]{:S(2)}) async-start(), calls=%async_computation.1 | async-start | bytes 7077888 | tf_op jit(solution)/shard_map/all_gather | solution.py:26
Sparse Core Ops, SparseCore 0:
  9.2 48.1 all-gather.2
where the time goes:
time: 254 us; the launch traced here: 253 us
  blocking collectives  50.4 us (20%)
  local copies, waits for them, and re-layouts  45.3 us (18%)
  matrix products  42.8 us (17%)
  waiting for transfers between devices  39.5 us (16%)
  loops' own time  36.9 us (15%)
  other arithmetic  24.3 us (10%)
  between operations  13.4 us (5%)
    all_to_all x1, blocking collectives, on_device(): lax.all_to_all(attended, 'tp', split_axis=0, concat_axis=1, tiled=True)  50.4 us
    all_gather x1, waiting for transfers between devices, on_device(): kv_bank = lax.all_gather(paired[None], 'cp', axis=0, tiled=True)  39.5 us
    another operation x1, loops' own time, on_device(): lax.fori_loop(0, stretch_span + 1, one_tile, start_state)  36.9 us
    dot_general x5, matrix products, one_tile(): jnp.einsum('cqhjk,ckhd->cqhjd', weights.astype(jnp.bfloat16), pieces[:, 1...  32.5 us
    reduce_sum x5, other arithmetic, one_tile(): new_sum = rescale * running_sum + jnp.sum(weights, axis=-1)  14.3 us
    dot_general x5, matrix products, one_tile(): jnp.einsum('cqhjd,ckhd->cqhjk', q_blocks, pieces[:, 0], preferred_element...  10.2 us
    reshape x1, local copies, waits for them, and re-layouts, on_device(): kv_bank = kv_bank.reshape(bank_slots, 2, 2, half_rows, kv_local, HEAD)  9.75 us
    unnamed x2, local copies, waits for them, and re-layouts  9.53 us
  transfers between devices with their start and end apart: 1, of which 1 were waited for; matrix products, arithmetic and copies ran while one was open for 4% of the time, Pallas kernels for 0%

commit v1 on v0

--- a/solution.py
+++ b/solution.py
@@ -81,7 +81,10 @@
     )
     final_max, final_sum, final_out = lax.fori_loop(0, stretch_span + 1, one_tile, start_state)
     attended = (final_out / final_sum[..., None]).reshape(tok_rows, q_cols).astype(jnp.bfloat16)
-    return lax.all_to_all(attended, "tp", split_axis=0, concat_axis=1, tiled=True)
+    return jnp.concatenate(
+        lax.all_to_all(jnp.stack(jnp.split(attended, lax.axis_size("tp"), axis=0)), "tp", 0, 0),
+        axis=1,
+    )
 
 
 def solution(mesh):

time: 254 us -> 252 us (level)
    convert_element_type x2 -> x1, local copies, waits for them, and re-layouts: 7.04 us -> 2.03 us  [on_device(): (final_out / final_sum[..., None]).reshape(tok_rows, q_cols)]
    another operation x0 -> x2, local copies, waits for them, and re-layouts: none -> 3.02 us  [on_device(): jnp.stack(jnp.split(attended, lax.axis_size('tp'), axis=0))]
    unnamed x2 -> x3, local copies, waits for them, and re-layouts: 9.53 us -> 9.92 us
where the time goes in v1:
time: 252 us; the launch traced here: 250 us
  blocking collectives  50.4 us (20%)
  local copies, waits for them, and re-layouts  43.7 us (17%)
  matrix products  42.8 us (17%)
  waiting for transfers between devices  39.5 us (16%)
  loops' own time  36.9 us (15%)
  other arithmetic  23.7 us (9%)
  between operations  13.5 us (5%)
    all_to_all x1, blocking collectives, on_device(): lax.all_to_all(jnp.stack(jnp.split(attended, lax.axis_size('tp'), axis=0)...  50.4 us
    all_gather x1, waiting for transfers between devices, on_device(): kv_bank = lax.all_gather(paired[None], 'cp', axis=0, tiled=True)  39.5 us
    another operation x1, loops' own time, on_device(): lax.fori_loop(0, stretch_span + 1, one_tile, start_state)  36.9 us
    dot_general x5, matrix products, one_tile(): jnp.einsum('cqhjk,ckhd->cqhjd', weights.astype(jnp.bfloat16), pieces[:, 1...  32.5 us
    reduce_sum x5, other arithmetic, one_tile(): new_sum = rescale * running_sum + jnp.sum(weights, axis=-1)  14.3 us
    dot_general x5, matrix products, one_tile(): jnp.einsum('cqhjd,ckhd->cqhjk', q_blocks, pieces[:, 0], preferred_element...  10.2 us
    unnamed x3, local copies, waits for them, and re-layouts  9.92 us
    reshape x1, local copies, waits for them, and re-layouts, on_device(): kv_bank = kv_bank.reshape(bank_slots, 2, 2, half_rows, kv_local, HEAD)  9.75 us
  transfers between devices with their start and end apart: 1, of which 1 were waited for; matrix products, arithmetic and copies ran while one was open for 4% of the time, Pallas kernels for 0%

profile of v1, /device:TPU:0, one launch (start us, length us, event | category | flops | bytes accessed | tf_op | source)
XLA Modules:
  0.0 250.5 jit_solution(3112192983296691636)
XLA Ops:
  6.5 2.1 pad_maximum_fusion.2
  8.7 0.8 reduce-window.8
  9.5 5.7 %reshape.171 = bf16[2,384,2,5,128]{4,3,2,1,0:T(8,128)(2,1)} reshape(bf16[768,1280]{1,0:T(8,128)(2,1)} %param.6) | data formatting | bytes 3932160 | tf_op jit(solution)/shard_map/reshape | solution.py:33
  15.2 2.4 copy.42
  17.6 0.1 broadcast_multiply_fusion.1
  17.7 0.1 iota_add_fusion.2
  17.8 0.1 convert_reduce_fusion.1
  17.9 39.5 %all-gather.3.cloned.1.call-done = bf16[16,768,256]{2,1,0:T(8,128)(2,1)} async-done(((bf16[2,768,256]{2,1,0:T(8,128)(2,1)}), bf16[16,768,256]{2,1,0:T(8,128)(2,1)}) %all-gather.3.cloned.1.call-update) | async-done | bytes 6291472 | tf_op jit(solution)/shard_map/all_gather | solution.py:26
  57.4 9.8 %reshape.163 = bf16[8,2,2,384,2,128]{5,4,3,2,1,0:T(2,128)(2,1)} reshape(bf16[16,768,256]{2,1,0:T(8,128)(2,1)} %all-gather.3.cloned.1.call-done) | data formatting | bytes 12582912 | tf_op jit(solution)/shard_map/reshape | solution.py:28
  67.1 7.1 %copy.41 = bf16[8,2,2,384,2,128]{5,3,4,1,2,0:T(8,128)(2,1)} copy(bf16[8,2,2,384,2,128]{5,4,3,2,1,0:T(2,128)(2,1)} %reshape.163) | data formatting | bytes 12582912
  74.2 108.8 %while.21 = (s32[]{:T(128)}, f32[2,384,2,5]{1,3,2,0:T(8,128)S(1)}, f32[2,384,2,5]{1,3,2,0:T(8,128)S(1)}, f32[2,384,2,5,128]{1,4,3,2,0:T(8,128)}, s32[2]{0:T(128)...) while((s32[]{:T(128)}, f32[2,384,2,5]{1,3,2,0:T(8,128)S(1)}, ...), condition=%wide.region_6.7_spmd.clone, body=%wide.region_2.6_spmd.clone.sunk | while | flops 1554047232 | bytes 50061820 | solution.py:82
  74.2 0.6 fusion.41
  78.5 0.6 fusion.40
  82.7 0.1 iota_add_fusion.4
  82.8 0.1 convert_reduce_fusion.3
  82.9 0.4 compare_and_fusion.2
  83.3 1.2 dynamic-slice_bitcast_fusion.3
  84.5 2.0 fusion.42
  86.5 2.9 %fusion.43 = f32[2,384,2,5]{1,3,2,0:T(8,128)S(1)} fusion(f32[2,2,384,384,5]{3,2,4,1,0:T(8,128)S(1)} %get-tuple-element.512, f32[2,384,2,5]{1,3,2,0:T(8,128)S(1)} %select_maximum_fusion.2, pred[2,384,384]{1,2,0:T(8,128)(4,1)S(1)} %compare_and_fusion.2), kind=kLoop, calls=%fused_computation.6.clone.1 | loop fusion | flops 14737920 | bytes 12152832 | tf_op jit(solution)/shard_map/while/body/eval_jaxpr/reduce_sum | solution.py:67
  89.4 5.3 %bitcast_add_fusion.2 = f32[2,384,2,5,128]{1,4,3,2,0:T(8,128)} fusion(f32[2,384,2,5,128]{1,4,3,2,0:T(8,128)} %get-tuple-element.533, f32[2,2,384,384,5]{3,2,4,1,0:T(8,128)S(1)} %get-tuple-element.512, f32[2,384,2,5]{1,3,2,0:T(8,128)S(1)} %select_maximum_fusion.2, pred[2,384,384]{1,2,0:T(8,128)(4,1)S(1)} %compare_and_fusion.2, ...), kind=kOutput, calls=%fused_computation.9.clone.1 | convolution fusion | flops 773455872 | bytes 20803584 | tf_op jit(solution)/shard_map/while/body/eval_jaxpr/cqhjk,ckhd->cqhjd/dot_general | solution.py:68
  94.8 0.6 fusion.41
  99.0 0.6 fusion.40
  103.3 0.1 iota_add_fusion.4
  103.4 0.1 convert_reduce_fusion.3
  103.4 0.4 compare_and_fusion.2
  103.8 1.2 dynamic-slice_bitcast_fusion.3
  105.0 2.0 fusion.42
  107.1 2.9 %fusion.43 = f32[2,384,2,5]{1,3,2,0:T(8,128)S(1)} fusion(f32[2,2,384,384,5]{3,2,4,1,0:T(8,128)S(1)} %get-tuple-element.512, f32[2,384,2,5]{1,3,2,0:T(8,128)S(1)} %select_maximum_fusion.2, pred[2,384,384]{1,2,0:T(8,128)(4,1)S(1)} %compare_and_fusion.2), kind=kLoop, calls=%fused_computation.6.clone.1 | loop fusion | flops 14737920 | bytes 12152832 | tf_op jit(solution)/shard_map/while/body/eval_jaxpr/reduce_sum | solution.py:67
  110.0 6.8 %bitcast_add_fusion.2 = f32[2,384,2,5,128]{1,4,3,2,0:T(8,128)} fusion(f32[2,384,2,5,128]{1,4,3,2,0:T(8,128)} %get-tuple-element.533, f32[2,2,384,384,5]{3,2,4,1,0:T(8,128)S(1)} %get-tuple-element.512, f32[2,384,2,5]{1,3,2,0:T(8,128)S(1)} %select_maximum_fusion.2, pred[2,384,384]{1,2,0:T(8,128)(4,1)S(1)} %compare_and_fusion.2, ...), kind=kOutput, calls=%fused_computation.9.clone.1 | convolution fusion | flops 773455872 | bytes 20803584 | tf_op jit(solution)/shard_map/while/body/eval_jaxpr/cqhjk,ckhd->cqhjd/dot_general | solution.py:68
  116.8 0.6 fusion.41
  121.1 0.6 fusion.40
  125.3 0.1 iota_add_fusion.4
  125.4 0.1 convert_reduce_fusion.3
  125.5 0.4 compare_and_fusion.2
  125.9 1.2 dynamic-slice_bitcast_fusion.3
  127.1 2.0 fusion.42
  129.1 2.9 %fusion.43 = f32[2,384,2,5]{1,3,2,0:T(8,128)S(1)} fusion(f32[2,2,384,384,5]{3,2,4,1,0:T(8,128)S(1)} %get-tuple-element.512, f32[2,384,2,5]{1,3,2,0:T(8,128)S(1)} %select_maximum_fusion.2, pred[2,384,384]{1,2,0:T(8,128)(4,1)S(1)} %compare_and_fusion.2), kind=kLoop, calls=%fused_computation.6.clone.1 | loop fusion | flops 14737920 | bytes 12152832 | tf_op jit(solution)/shard_map/while/body/eval_jaxpr/reduce_sum | solution.py:67
  132.1 6.8 %bitcast_add_fusion.2 = f32[2,384,2,5,128]{1,4,3,2,0:T(8,128)} fusion(f32[2,384,2,5,128]{1,4,3,2,0:T(8,128)} %get-tuple-element.533, f32[2,2,384,384,5]{3,2,4,1,0:T(8,128)S(1)} %get-tuple-element.512, f32[2,384,2,5]{1,3,2,0:T(8,128)S(1)} %select_maximum_fusion.2, pred[2,384,384]{1,2,0:T(8,128)(4,1)S(1)} %compare_and_fusion.2, ...), kind=kOutput, calls=%fused_computation.9.clone.1 | convolution fusion | flops 773455872 | bytes 20803584 | tf_op jit(solution)/shard_map/while/body/eval_jaxpr/cqhjk,ckhd->cqhjd/dot_general | solution.py:68
  138.9 0.6 fusion.41
  143.2 0.6 fusion.40
  147.4 0.1 iota_add_fusion.4
  147.5 0.1 convert_reduce_fusion.3
  147.6 0.4 compare_and_fusion.2
  148.0 1.2 dynamic-slice_bitcast_fusion.3
  149.1 2.0 fusion.42
  151.2 2.9 %fusion.43 = f32[2,384,2,5]{1,3,2,0:T(8,128)S(1)} fusion(f32[2,2,384,384,5]{3,2,4,1,0:T(8,128)S(1)} %get-tuple-element.512, f32[2,384,2,5]{1,3,2,0:T(8,128)S(1)} %select_maximum_fusion.2, pred[2,384,384]{1,2,0:T(8,128)(4,1)S(1)} %compare_and_fusion.2), kind=kLoop, calls=%fused_computation.6.clone.1 | loop fusion | flops 14737920 | bytes 12152832 | tf_op jit(solution)/shard_map/while/body/eval_jaxpr/reduce_sum | solution.py:67
  154.1 6.8 %bitcast_add_fusion.2 = f32[2,384,2,5,128]{1,4,3,2,0:T(8,128)} fusion(f32[2,384,2,5,128]{1,4,3,2,0:T(8,128)} %get-tuple-element.533, f32[2,2,384,384,5]{3,2,4,1,0:T(8,128)S(1)} %get-tuple-element.512, f32[2,384,2,5]{1,3,2,0:T(8,128)S(1)} %select_maximum_fusion.2, pred[2,384,384]{1,2,0:T(8,128)(4,1)S(1)} %compare_and_fusion.2, ...), kind=kOutput, calls=%fused_computation.9.clone.1 | convolution fusion | flops 773455872 | bytes 20803584 | tf_op jit(solution)/shard_map/while/body/eval_jaxpr/cqhjk,ckhd->cqhjd/dot_general | solution.py:68
  161.0 0.6 fusion.41
  165.2 0.6 fusion.40
  169.5 0.1 iota_add_fusion.4
  169.5 0.1 convert_reduce_fusion.3
  169.6 0.4 compare_and_fusion.2
  170.0 1.2 dynamic-slice_bitcast_fusion.3
  171.2 2.0 fusion.42
  173.3 2.9 %fusion.43 = f32[2,384,2,5]{1,3,2,0:T(8,128)S(1)} fusion(f32[2,2,384,384,5]{3,2,4,1,0:T(8,128)S(1)} %get-tuple-element.512, f32[2,384,2,5]{1,3,2,0:T(8,128)S(1)} %select_maximum_fusion.2, pred[2,384,384]{1,2,0:T(8,128)(4,1)S(1)} %compare_and_fusion.2), kind=kLoop, calls=%fused_computation.6.clone.1 | loop fusion | flops 14737920 | bytes 12152832 | tf_op jit(solution)/shard_map/while/body/eval_jaxpr/reduce_sum | solution.py:67
  176.2 6.8 %bitcast_add_fusion.2 = f32[2,384,2,5,128]{1,4,3,2,0:T(8,128)} fusion(f32[2,384,2,5,128]{1,4,3,2,0:T(8,128)} %get-tuple-element.533, f32[2,2,384,384,5]{3,2,4,1,0:T(8,128)S(1)} %get-tuple-element.512, f32[2,384,2,5]{1,3,2,0:T(8,128)S(1)} %select_maximum_fusion.2, pred[2,384,384]{1,2,0:T(8,128)(4,1)S(1)} %compare_and_fusion.2, ...), kind=kOutput, calls=%fused_computation.9.clone.1 | convolution fusion | flops 773455872 | bytes 20803584 | tf_op jit(solution)/shard_map/while/body/eval_jaxpr/cqhjk,ckhd->cqhjd/dot_general | solution.py:68
  183.0 2.5 %divide_convert_fusion = bf16[2,384,2,5,128]{1,4,3,2,0:T(8,128)(2,1)S(1)} fusion(f32[2,384,2,5,128]{1,4,3,2,0:T(8,128)} %get-tuple-element.300, f32[2,384,2,5]{1,3,2,0:T(8,128)S(1)} %get-tuple-element.301), kind=kLoop, calls=%fused_computation.40 | loop fusion | flops 1966080 | bytes 5928960 | tf_op jit(solution)/shard_map/convert_element_type | solution.py:83
  185.6 2.0 copy.43
  187.6 0.4 copy.57
  188.0 0.6 slice_bitcast_fusion.3
  188.6 0.7 pad_maximum_fusion.1
  189.3 2.4 copy.46
  191.7 50.4 %all_to_all.5 = bf16[4,192,1280]{2,1,0:T(8,128)(2,1)S(1)} all-to-all(bf16[4,192,1280]{2,1,0:T(8,128)(2,1)} %copy.46), channel_id=1, replica_groups=mesh['cp'=8,'tp'=4] {'tp'}, dimensions={0} | all-to-all | bytes 3932160 | tf_op jit(solution)/shard_map/all_to_all | solution.py:85
  242.1 1.5 copy.56
  (30 shorter events, 0.4 us)
Async XLA Ops:
  6.5 50.8 %all-gather.3.cloned.1.call-start = ((), (), s32[]{:S(2)}) async-start(), calls=%async_computation.1 | async-start | bytes 7077888 | tf_op jit(solution)/shard_map/all_gather | solution.py:26
Sparse Core Ops, SparseCore 0:
  9.2 48.1 all-gather.2
